TPU v7x, 8 devices: a whole 2x2x1 slice. The times are simulated.
8 devices in a mesh: dp: 2 (over y, z), sp: 4 (over x, core).
Axes of the slice: x: 2, y: 2, z: 1, core: 2. Of those that a mesh axis runs over, the one named last changes fastest.
Arguments:
- q: bfloat16 [64, 80, 80], P('dp'), parts along dimension 0
- k: bfloat16 [64, 8192, 8, 80], P('dp', 'sp'), parts along dimension 0
- v: bfloat16 [64, 8192, 8, 80], P('dp', 'sp'), parts along dimension 0
Outputs:
- q: bfloat16 [64, 80, 80], P('dp'), parts along dimension 0
There are 2 independent parts. A program takes and returns all parts, laid end to end along the dimension named above; each array names one.
All inputs are finite; a program needn't handle non-finite values.
Results may differ from a plain program's by a relative error of at most 0.012.
Values are sent between devices in bfloat16 or wider.
A program may use at most 2 GiB of HBM per device.

v0:
```python
import jax
import jax.numpy as jnp
from jax import lax
from jax.sharding import PartitionSpec as P


def einsum(form, a, b):
    return jnp.einsum(form, a.astype(jnp.float32), b.astype(jnp.float32))


def part_of(q, k, v):
    grouped = q.reshape(q.shape[0], k.shape[2], -1, q.shape[2])
    scores = einsum("bgsd,bugd->bgsu", grouped, k) * q.shape[2] ** -0.5
    high = jnp.max(scores, -1, keepdims=True)
    weights = jnp.exp(scores - high)
    seen = einsum("bgsu,bugd->bgsd", weights.astype(jnp.bfloat16), v)
    return jnp.concatenate([seen, jnp.sum(weights, -1, keepdims=True), high], -1)


def together(parts):
    seen, total, high = parts[..., :-2], parts[..., -2:-1], parts[..., -1:]
    scale = jnp.exp(high - jnp.max(high, 0))
    return (jnp.sum(seen * scale, 0) / jnp.sum(total * scale, 0)).astype(jnp.bfloat16)


def solution(mesh):
    def step(q, k, v):
        return together(lax.all_gather(part_of(q, k, v), "sp")).reshape(q.shape)

    return jax.shard_map(
        step,
        mesh=mesh,
        in_specs=(P("dp", None, None), P("dp", "sp", None, None), P("dp", "sp", None, None)),
        out_specs=P("dp", None, None),
        check_vma=False,
    )
```

profile of v0, /device:TPU:0, one launch (start us, length us, event | category | flops | bytes accessed | tf_op | source)
XLA Modules:
  0.0 183.1 jit_solution(17305441260897771998)
XLA Ops:
  6.5 0.0 all-gather.3.cloned.1.call-start
  6.5 1.3 copy.38
  7.8 39.8 %multiply_reduce_fusion = (f32[32,8,10]{2,1,0:T(8,128)S(1)}, f32[32,8,10,2048]{3,2,1,0:T(8,128)}) fusion(bf16[32,2048,8,80]{1,3,2,0:T(8,128)(2,1)} %param.4, bf16[32,8,10,80]{3,0,2,1:T(8,128)(2,1)S(1)} %bitcast.17), kind=kOutput, calls=%fused_computation.1 | convolution fusion | flops 849344000 | bytes 105277440 | tf_op jit(solution)/shard_map/bgsd,bugd->bgsu/dot_general | solution.py:8
  47.6 14.2 %fusion = f32[32,8,10]{2,1,0:T(8,128)S(1)} fusion(f32[32,8,10,2048]{3,2,1,0:T(8,128)} %get-tuple-element.11, f32[32,8,10]{2,1,0:T(8,128)S(1)} %get-tuple-element.10), kind=kLoop, calls=%fused_computation.2 | loop fusion | flops 15726080 | bytes 20992000 | tf_op jit(solution)/shard_map/reduce_sum | solution.py:17
  61.8 37.6 %fusion.2 = f32[32,8,10,80]{3,2,1,0:T(8,128)S(1)} fusion(bf16[32,2048,8,80]{1,3,2,0:T(8,128)(2,1)} %param.5, f32[32,8,10,2048]{3,2,1,0:T(8,128)} %get-tuple-element.11, f32[32,8,10]{2,1,0:T(8,128)S(1)} %get-tuple-element.10), kind=kOutput, calls=%fused_computation.4 | convolution fusion | flops 854589440 | bytes 105687040 | tf_op jit(solution)/shard_map/bgsu,bugd->bgsd/dot_general | solution.py:8
  99.4 3.0 %copy.42 = f32[32,8,10,1]{3,2,1,0:T(8,128)} copy(f32[32,8,10,1]{2,1,0,3:T(8,128)S(1)} %bitcast.19) | data formatting | bytes 20480 | tf_op jit(solution)/shard_map/broadcast_in_dim | solution.py:17
  102.4 3.0 %copy.43 = f32[32,8,10,1]{3,2,1,0:T(8,128)} copy(f32[32,8,10,1]{2,1,0,3:T(8,128)S(1)} %bitcast.18) | data formatting | bytes 20480 | tf_op jit(solution)/shard_map/broadcast_in_dim | solution.py:14
  105.4 3.4 %pad_maximum_fusion = f32[32,8,10,82]{3,2,1,0:T(8,128)S(1)} fusion(f32[32,8,10,1]{3,2,1,0:T(8,128)} %copy.43, f32[32,8,10,1]{3,2,1,0:T(8,128)} %copy.42, f32[32,8,10,80]{3,2,1,0:T(8,128)S(1)} %fusion.2), kind=kLoop, calls=%fused_computation.9 | loop fusion | flops 419840 | bytes 1679360 | tf_op jit(solution)/shard_map/concatenate | solution.py:17
  108.8 1.7 copy.44
  110.4 0.0 all-gather.3.cloned.1.call-update
  110.5 40.5 %all-gather.3.cloned.1.call-done = f32[128,8,10,82]{3,1,2,0:T(8,128)} async-done(((f32[32,8,10,82]{3,1,2,0:T(8,128)}), f32[128,8,10,82]{3,1,2,0:T(8,128)}) %all-gather.3.cloned.1.call-update) | async-done | bytes 3358736 | tf_op jit(solution)/shard_map/all_gather | solution.py:28
  151.0 10.8 %fusion.12 = (f32[4,32,8,10,1]{4,2,3,1,0:T(8,128)}, f32[32,8,10]{1,2,0:T(8,128)S(1)}, f32[4,32,8,10,1]{4,2,3,1,0:T(8,128)}) fusion(f32[4,32,8,10,82]{4,2,3,1,0:T(8,128)} %bitcast.15), kind=kLoop, calls=%fused_computation.19 | loop fusion | flops 7680 | bytes 174080 | tf_op jit(solution)/shard_map/slice | solution.py:21
  161.8 3.8 %copy.58 = f32[4,32,8,10,1]{1,2,4,3,0:T(8,128)S(1)} copy(f32[4,32,8,10,1]{4,2,3,1,0:T(8,128)} %get-tuple-element.5) | data formatting | bytes 81920
  165.6 0.1 copy.60
  165.7 3.8 %copy.57 = f32[4,32,8,10,1]{1,2,4,3,0:T(8,128)S(1)} copy(f32[4,32,8,10,1]{4,2,3,1,0:T(8,128)} %get-tuple-element.7) | data formatting | bytes 81920
  169.5 0.5 copy.46
  170.0 4.3 %fusion.6 = f32[32,8,10,80]{3,1,2,0:T(8,128)S(1)} fusion(f32[4,32,8,10,82]{4,2,3,1,0:T(8,128)} %bitcast.16, f32[4,32,8,10]{2,3,1,0:T(8,128)S(1)} %copy.46), kind=kLoop, calls=%fused_computation.8 | loop fusion | flops 1433600 | bytes 4136960 | tf_op jit(solution)/shard_map/reduce_sum | solution.py:23
  174.3 0.4 copy.48
  174.7 0.4 fusion.7
  175.2 1.1 copy.51
  (3 shorter events, 0.1 us)
Async XLA Ops:
  6.5 144.5 %all-gather.3.cloned.1.call-start = ((), (), s32[]{:S(2)}) async-start(), calls=%async_computation | async-start | bytes 6553600 | tf_op jit(solution)/shard_map/all_gather | solution.py:28
Sparse Core Ops, SparseCore 0:
  110.6 40.3 all-gather.2
where the time goes:
time: 183 us
  matrix products  77.4 us (42%)
  waiting for transfers between devices  40.6 us (22%)
  other arithmetic  33.1 us (18%)
  local copies, waits for them, and re-layouts  18.6 us (10%)
  between operations  13.5 us (7%)
    dot_general x2, matrix products, einsum(): return jnp.einsum(form, a.astype(jnp.float32), b.astype(jnp.float32))  77.4 us
    all_gather x1, waiting for transfers between devices, step(): return together(lax.all_gather(part_of(q, k, v), 'sp')).reshape(q.shape)  40.5 us
    reduce_sum x1, other arithmetic, part_of(): jnp.sum(weights, -1, keepdims=True)  14.2 us
    slice x1, other arithmetic, together(): seen, total, high = (parts[..., :-2], parts[..., -2:-1], parts[..., -1:])  10.8 us
    unnamed x4, local copies, waits for them, and re-layouts  8.93 us
    reduce_sum x1, other arithmetic, together(): jnp.sum(seen * scale, 0) / jnp.sum(total * scale, 0)  4.26 us
  transfers between devices with their start and end apart: 1, of which 1 were waited for; matrix products, arithmetic and copies ran while one was open for 0% of the time, Pallas kernels for 0%

commit v1 on v0

v1 whole, which is shorter than its diff:
```python
import math

import jax
import jax.numpy as jnp
from jax import lax
from jax.experimental import pallas as pl
from jax.experimental.pallas import tpu as pltpu
from jax.sharding import PartitionSpec as P

KDEPTH, VDEPTH = 4, 4
WAIT = 3
RING = 10
PAD = 256
TILE = 256
F32, BF16 = jnp.float32, jnp.bfloat16
MESH = pl.DeviceIdType.MESH


def kernel(n, groups, share, q_hbm, k_hbm, v_hbm, out_ref, q_ref, kbuf, vbuf, spread, pick, qbd0, qbd1, s0, s1, p0, p1, parts, stats, tally, qsem, ksem, vsem, send_sem, recv_sem):
    count, heads, head = q_ref.shape
    rows, run = k_hbm.shape[1], k_hbm.shape[2]
    half = rows // 2
    factor = head**-0.5 * math.log2(math.e)
    me = lax.axis_index("sp")
    peers = [lax.rem(me + d, n) for d in range(1, n)]
    qbd, score, prob = (qbd0, qbd1), (s0, s1), (p0, p1)

    def keys(i):
        slot = lax.rem(i, KDEPTH)
        return pltpu.make_async_copy(k_hbm.at[i], kbuf.at[slot, :, :run], ksem.at[slot])

    def values(i):
        slot = lax.rem(i, VDEPTH)
        return pltpu.make_async_copy(v_hbm.at[i], vbuf.at[slot, :, :run], vsem.at[slot])

    def sends(i):
        slot = lax.rem(i, RING)
        return [
            pltpu.make_async_remote_copy(
                src_ref=ref.at[me, slot],
                dst_ref=ref.at[me, slot],
                send_sem=send_sem.at[slot],
                recv_sem=recv_sem.at[slot],
                device_id={"sp": peer},
                device_id_type=MESH,
            )
            for peer in peers
            for ref in (parts, stats)
        ]

    def arrive(i):
        for sem in (send_sem, recv_sem):
            pltpu.make_async_copy(tally, tally, sem.at[lax.rem(i, RING)]).wait()

    def widen(i, side):
        wide = jnp.dot(q_ref[i], spread[...], preferred_element_type=F32).astype(BF16)
        qbd[side][...] = wide * pick[...]

    def together(i):
        slot = lax.rem(i, RING)
        high = [stats[d, slot, 0:1, :heads] for d in range(n)]
        total = [stats[d, slot, 1:2, :heads] for d in range(n)]
        top = high[0]
        for h in high[1:]:
            top = jnp.maximum(top, h)
        scale = [jnp.exp2((h - top) * factor) for h in high]
        whole = total[0] * scale[0]
        for t, c in zip(total[1:], scale[1:]):
            whole += t * c
        acc = parts[0, slot, :, :heads].astype(F32) * scale[0]
        for d in range(1, n):
            acc += parts[d, slot, :, :heads].astype(F32) * scale[d]
        out_ref[i] = (acc / whole).T.astype(BF16)

    def block(scores=None, soften=None, add=None):
        if soften is not None:
            s_in, p_out = soften[1:]
            high = s_in[:, :128]
            for c in range(128, run, 128):
                high = jnp.maximum(high, s_in[:, c : c + 128])
            high = jnp.max(high, -1, keepdims=True)
            total = jnp.zeros((heads, 128), F32)
        seen = {}
        for t in range(0, run, TILE):
            tile = slice(t, t + TILE)
            if add is not None:
                for a in range(2):
                    v = vbuf[lax.rem(add[0], VDEPTH), a * half : (a + 1) * half, tile]
                    d = lax.dot_general(v, add[1][:, tile], (((1,), (1,)), ((), ())), preferred_element_type=F32)
                    seen[a] = seen[a] + d if a in seen else d
            if scores is not None:
                i, q_in, s_out = scores
                s_out[:, tile] = jnp.dot(q_in[...], kbuf[lax.rem(i, KDEPTH), :, tile], preferred_element_type=F32)
            if soften is not None:
                p = jnp.exp2((s_in[:, tile] - high) * factor)
                p_out[:, tile] = p.astype(BF16)
                for c in range(0, TILE, 128):
                    total += p[:, c : c + 128]
        if soften is not None:
            total = jnp.sum(total, -1, keepdims=True)
            spot = lax.broadcasted_iota(jnp.int32, (heads, 128), 1)
            both = jnp.where(spot == 0, high, total)
            stats[me, lax.rem(soften[0], RING), :, :heads] = both.T[:2]
        if add is not None:
            column = lax.broadcasted_iota(jnp.int32, (head, heads), 1)
            part = jnp.zeros((head, heads), F32)
            for a in range(2):
                for b in range(groups // 2):
                    g = a * groups // 2 + b
                    here = (column >= g * share) & (column < (g + 1) * share)
                    part = jnp.where(here, seen[a][b * head : (b + 1) * head], part)
            parts[me, lax.rem(add[0], RING), :, :heads] = part.astype(BF16)

    def start(i):
        @pl.when(i - 1 + KDEPTH < count)
        def _():
            keys(i - 1 + KDEPTH).start()

        @pl.when(i - 3 + VDEPTH < count)
        def _():
            values(i - 3 + VDEPTH).start()

    def step(i, a, late, first=False):
        if first:

            @pl.when(i >= 3)
            def _():
                start(i)
                for copy in sends(i - 3):
                    copy.start()

            @pl.when(i < 3)
            def _():
                keys(i - 1 + KDEPTH).start()
        else:
            start(i)
            for copy in sends(i - 3):
                copy.start()
        if late:
            arrive(i - 3 - WAIT)
        keys(i).wait()
        values(i - 2).wait()
        if late:
            together(i - 3 - WAIT)
        widen(jnp.minimum(i + 1, count - 1), 1 - a)
        block((i, qbd[a], score[a]), (i - 1, score[1 - a], prob[1 - a]), (i - 2, prob[a]))

    keys(0).start()
    pltpu.make_async_copy(q_hbm, q_ref, qsem).start()
    for i in range(1, VDEPTH + 2):
        if i < KDEPTH:
            keys(i).start()
        if i >= 2:
            values(i - 2).start()

    barrier = pltpu.get_barrier_semaphore()
    for peer in peers:
        pl.semaphore_signal(barrier, inc=1, device_id={"sp": peer}, device_id_type=MESH)

    lane = lax.broadcasted_iota(jnp.int32, (head, rows), 1)
    row = lax.broadcasted_iota(jnp.int32, (head, rows), 0)
    spread[...] = (lax.rem(lane, head) == row).astype(F32).astype(BF16)
    lane = lax.broadcasted_iota(jnp.int32, (heads, rows), 1)
    row = lax.broadcasted_iota(jnp.int32, (heads, rows), 0)
    pick[...] = (lane // head == row // share).astype(F32).astype(BF16)

    pltpu.make_async_copy(q_hbm, q_ref, qsem).wait()
    widen(0, 0)
    widen(1, 1)
    keys(0).wait()
    block((0, qbd0, s0))
    keys(KDEPTH).start()
    keys(1).wait()
    widen(2, 0)
    block((1, qbd1, s1), (0, s0, p0))
    pl.semaphore_wait(barrier, n - 1)

    def pair(late, first, j, carry):
        step(2 * j, 0, late, first)
        step(2 * j + 1, 1, late)
        return carry

    lax.fori_loop(1, 3, lambda j, c: pair(False, True, j, c), 0)
    lax.fori_loop(3, count // 2, lambda j, c: pair(True, False, j, c), 0)

    last = count - 1
    for copy in sends(last - 2):
        copy.start()
    values(last - 1).wait()
    block(None, (last, s1, p1), (last - 1, p0))
    for copy in sends(last - 1):
        copy.start()
    values(last).wait()
    block(None, None, (last, p1))
    for copy in sends(last):
        copy.start()

    def rest(i, carry):
        arrive(i)
        together(i)
        return carry

    lax.fori_loop(last - 2 - WAIT, count, rest, 0)


def solution(mesh):
    n = mesh.shape["sp"]

    def step(q, k, v):
        count, run, groups, head = k.shape
        heads = q.shape[1]
        rows = groups * head
        k, v = (a.transpose(0, 2, 3, 1).reshape(count, rows, run) for a in (k, v))

        def body(*refs):
            kernel(n, groups, heads // groups, *refs)

        return pl.pallas_call(
            body,
            out_shape=jax.ShapeDtypeStruct((count, heads, head), BF16),
            in_specs=[pl.BlockSpec(memory_space=pl.ANY)] * 3,
            out_specs=pl.BlockSpec(memory_space=pltpu.VMEM),
            scratch_shapes=[
                pltpu.VMEM((count, heads, head), BF16),
                pltpu.VMEM((KDEPTH, rows, run + PAD), BF16),
                pltpu.VMEM((VDEPTH, rows, run + PAD), BF16),
                pltpu.VMEM((head, rows), BF16),
                pltpu.VMEM((heads, rows), BF16),
                pltpu.VMEM((heads, rows), BF16),
                pltpu.VMEM((heads, rows), BF16),
                pltpu.VMEM((heads, run), F32),
                pltpu.VMEM((heads, run), F32),
                pltpu.VMEM((heads, run), BF16),
                pltpu.VMEM((heads, run), BF16),
                pltpu.VMEM((n, RING, head, 128), BF16),
                pltpu.VMEM((n, RING, 2, 128), F32),
                pltpu.VMEM((n - 1, head // 2 + 2, 128), F32),
                pltpu.SemaphoreType.DMA,
                pltpu.SemaphoreType.DMA((KDEPTH,)),
                pltpu.SemaphoreType.DMA((VDEPTH,)),
                pltpu.SemaphoreType.DMA((RING,)),
                pltpu.SemaphoreType.DMA((RING,)),
            ],
            compiler_params=pltpu.CompilerParams(
                collective_id=0, has_side_effects=True, vmem_limit_bytes=54125 * 1024
            ),
        )(q, k, v)

    return jax.shard_map(
        step,
        mesh=mesh,
        in_specs=(P("dp", None, None), P("dp", "sp", None, None), P("dp", "sp", None, None)),
        out_specs=P("dp", None, None),
        check_vma=False,
    )
```

time: 183 us -> 57.7 us (0.32)
  matrix products: 77.4 us -> 0 us
  Pallas kernels: 0 us -> 56.7 us
  waiting for transfers between devices: 40.6 us -> 0 us
  other arithmetic: 33.1 us -> 0 us
  local copies, waits for them, and re-layouts: 18.6 us -> 0.84 us
  between operations: 13.5 us -> 0.01 us
    dot_general x2 -> x0, matrix products: 77.4 us -> none  [einsum(): return jnp.einsum(form, a.astype(jnp.float32), b.astype(jnp.float32))]
    pallas_call x0 -> x1, Pallas kernels: none -> 56.7 us  [step(): pl.pallas_call(body, out_shape=jax.ShapeDtypeStruct((count, heads, head),...]
    all_gather x1 -> x0, waiting for transfers between devices: 40.5 us -> none  [step(): return together(lax.all_gather(part_of(q, k, v), 'sp')).reshape(q.shape)]
    reduce_sum x3 -> x0, other arithmetic: 18.5 us -> none  [the longest x1 14.2 us: part_of(): jnp.sum(weights, -1, keepdims=True)]
    slice x1 -> x0, other arithmetic: 10.8 us -> none  [together(): seen, total, high = (parts[..., :-2], parts[..., -2:-1], parts[..., -1:])]
    unnamed x4 -> x1, local copies, waits for them, and re-layouts: 8.93 us -> 0.84 us
    broadcast_in_dim x2 -> x0, local copies, waits for them, and re-layouts: 5.97 us -> none  [the longest x1 3.01 us: part_of(): high = jnp.max(scores, -1, keepdims=True)]
    concatenate x1 -> x0, other arithmetic: 3.37 us -> none  [part_of(): jnp.concatenate([seen, jnp.sum(weights, -1, keepdims=True), high], -1)]
  transfers between devices with their start and end apart: 1 -> 0, of which waited for: 1 -> 0; matrix products, arithmetic and copies ran while one was open for 0% -> 0% of each run, Pallas kernels for 0% -> 0%
where the time goes in v1:
time: 57.7 us; the launch traced here: 57.6 us
  Pallas kernels  56.7 us (98%)
  local copies, waits for them, and re-layouts  0.84 us (1%)
    pallas_call x1, Pallas kernels, step(): pl.pallas_call(body, out_shape=jax.ShapeDtypeStruct((count, heads, head),...  56.7 us

profile of v1, /device:TPU:0, one launch (start us, length us, event | category | flops | bytes accessed | tf_op | source)
XLA Modules:
  0.0 57.6 jit_solution(12658665324018581845)
XLA Ops:
  0.0 56.7 %shard_map.37 = bf16[32,80,80]{2,1,0:T(8,128)(2,1)S(1)} custom-call(bf16[32,80,80]{2,1,0:T(8,128)(2,1)} %refs_0_.1, bf16[32,640,2048]{2,1,0:T(8,128)(2,1)} %bitcast.1.refs_1_, bf16[32,640,2048]{2,1,0:T(8,128)(2,1)} %bitcast.3.refs_2_), custom_call_target="tpu_custom_call" | custom-call | tf_op jit(solution)/shard_map/pallas_call | solution.py:218
  56.8 0.8 %copy.5 = bf16[32,80,80]{2,1,0:T(8,128)(2,1)} copy(bf16[32,80,80]{2,1,0:T(8,128)(2,1)S(1)} %shard_map.37) | data formatting | bytes 819200

commit v2 on v1

--- a/solution.py
+++ b/solution.py
@@ -9,9 +9,10 @@
 
 KDEPTH, VDEPTH = 4, 4
 WAIT = 3
-RING = 10
+RING = 12
 PAD = 256
 TILE = 256
+AHEAD = 4 * TILE
 F32, BF16 = jnp.float32, jnp.bfloat16
 MESH = pl.DeviceIdType.MESH
 
@@ -72,7 +73,7 @@
             acc += parts[d, slot, :, :heads].astype(F32) * scale[d]
         out_ref[i] = (acc / whole).T.astype(BF16)
 
-    def block(scores=None, soften=None, add=None):
+    def block(scores=None, soften=None, add=None, ahead=0):
         if soften is not None:
             s_in, p_out = soften[1:]
             high = s_in[:, :128]
@@ -81,6 +82,16 @@
             high = jnp.max(high, -1, keepdims=True)
             total = jnp.zeros((heads, 128), F32)
         seen = {}
+
+        def mark(t):
+            tile = slice(t, t + TILE)
+            i, q_in, s_out = scores
+            s_out[:, tile] = jnp.dot(q_in[...], kbuf[lax.rem(i, KDEPTH), :, tile], preferred_element_type=F32)
+
+        for t in range(0, ahead, TILE):
+            mark(t)
+        if ahead:
+            values(add[0]).wait()
         for t in range(0, run, TILE):
             tile = slice(t, t + TILE)
             if add is not None:
@@ -88,9 +99,8 @@
                     v = vbuf[lax.rem(add[0], VDEPTH), a * half : (a + 1) * half, tile]
                     d = lax.dot_general(v, add[1][:, tile], (((1,), (1,)), ((), ())), preferred_element_type=F32)
                     seen[a] = seen[a] + d if a in seen else d
-            if scores is not None:
-                i, q_in, s_out = scores
-                s_out[:, tile] = jnp.dot(q_in[...], kbuf[lax.rem(i, KDEPTH), :, tile], preferred_element_type=F32)
+            if scores is not None and t >= ahead:
+                mark(t)
             if soften is not None:
                 p = jnp.exp2((s_in[:, tile] - high) * factor)
                 p_out[:, tile] = p.astype(BF16)
@@ -181,9 +191,17 @@
         return carry
 
     lax.fori_loop(1, 3, lambda j, c: pair(False, True, j, c), 0)
-    lax.fori_loop(3, count // 2, lambda j, c: pair(True, False, j, c), 0)
+    lax.fori_loop(3, count // 2 - 1, lambda j, c: pair(True, False, j, c), 0)
 
     last = count - 1
+    values(last).start()
+    for i, a in ((last - 1, 0), (last, 1)):
+        for copy in sends(i - 3):
+            copy.start()
+        keys(i).wait()
+        if i < last:
+            widen(last, 1)
+        block((i, qbd[a], score[a]), (i - 1, score[1 - a], prob[1 - a]), (i - 2, prob[a]), AHEAD)
     for copy in sends(last - 2):
         copy.start()
     values(last - 1).wait()
@@ -200,7 +218,7 @@
         together(i)
         return carry
 
-    lax.fori_loop(last - 2 - WAIT, count, rest, 0)
+    lax.fori_loop(last - 4 - WAIT, count, rest, 0)
 
 
 def solution(mesh):

time: 57.7 us -> 57.5 us (level)
  no operation moved by 1% of the time
where the time goes in v2:
time: 57.5 us; the launch traced here: 57.4 us
  Pallas kernels  56.6 us (98%)
  local copies, waits for them, and re-layouts  0.84 us (1%)
    pallas_call x1, Pallas kernels, step(): pl.pallas_call(body, out_shape=jax.ShapeDtypeStruct((count, heads, head),...  56.6 us

profile of v2, /device:TPU:0, one launch (start us, length us, event | category | flops | bytes accessed | tf_op | source)
XLA Modules:
  0.0 57.4 jit_solution(9856053702044515898)
XLA Ops:
  0.0 56.6 %shard_map.37 = bf16[32,80,80]{2,1,0:T(8,128)(2,1)S(1)} custom-call(bf16[32,80,80]{2,1,0:T(8,128)(2,1)} %refs_0_.1, bf16[32,640,2048]{2,1,0:T(8,128)(2,1)} %bitcast.1.refs_1_, bf16[32,640,2048]{2,1,0:T(8,128)(2,1)} %bitcast.3.refs_2_), custom_call_target="tpu_custom_call" | custom-call | tf_op jit(solution)/shard_map/pallas_call | solution.py:236
  56.6 0.8 %copy.5 = bf16[32,80,80]{2,1,0:T(8,128)(2,1)} copy(bf16[32,80,80]{2,1,0:T(8,128)(2,1)S(1)} %shard_map.37) | data formatting | bytes 819200
